TPU v7x, 8 devices: a whole 2x2x1 slice. The times are simulated.
8 devices in a mesh: data: 1 (over z), cp: 8 (over y, x, core).
Axes of the slice: x: 2, y: 2, z: 1, core: 2. Of those that a mesh axis runs over, the one named last changes fastest.
Arguments:
- q: bfloat16 [1, 4096, 96, 128], P('data', 'cp')
- k: bfloat16 [1, 4096, 96, 128], P('data', 'cp')
- v: bfloat16 [1, 4096, 96, 128], P('data', 'cp')
- o: bfloat16 [1, 4096, 96, 128], P('data', 'cp')
- lse: float32 [1, 96, 4096], P('data', None, 'cp')
- do: bfloat16 [1, 4096, 96, 128], P('data', 'cp')
Outputs:
- output 1: bfloat16 [1, 4096, 96, 128], P('data', 'cp')
- output 2: bfloat16 [1, 4096, 96, 128], P('data', 'cp')
- output 3: bfloat16 [1, 4096, 96, 128], P('data', 'cp')
All inputs are finite; a program needn't handle non-finite values.
Results may differ from a plain program's by a relative error of at most 0.001.
Values are sent between devices in bfloat16 or wider.
A program may use at most 1 GiB of HBM per device.

v0:
```python
import jax
import jax.numpy as jnp
from jax import lax
from jax.sharding import PartitionSpec as P

F32 = jnp.float32
BF16 = jnp.bfloat16


def _pair(q, do, lse, delta, k, v, mask, scale):
    s = jnp.einsum('bqhd,bkhd->bhqk', q, k, preferred_element_type=F32) * scale
    p = jnp.exp(s - lse[..., None])
    if mask is not None:
        p = jnp.where(mask, p, 0.0)
    dv = jnp.einsum('bhqk,bqhd->bkhd', p.astype(BF16), do, preferred_element_type=F32)
    dp = jnp.einsum('bqhd,bkhd->bhqk', do, v, preferred_element_type=F32)
    ds = (p * (dp - delta[..., None])).astype(BF16)
    dq = jnp.einsum('bhqk,bkhd->bqhd', ds, k, preferred_element_type=F32) * scale
    dk = jnp.einsum('bhqk,bqhd->bkhd', ds, q, preferred_element_type=F32) * scale
    return dq, dk, dv


def _same(q, do, lse, delta, k, v):
    c = q.shape[1] // 2
    scale = q.shape[-1] ** -0.5
    tri = jnp.tril(jnp.ones((c, c), bool))
    full = jnp.concatenate([jnp.ones((c, c), bool), tri], axis=1)
    dq0, dk0, dv0 = _pair(q[:, :c], do[:, :c], lse[..., :c], delta[..., :c], k[:, :c], v[:, :c], tri, scale)
    dq1, dk1, dv1 = _pair(q[:, c:], do[:, c:], lse[..., c:], delta[..., c:], k, v, full, scale)
    return jnp.concatenate([dq0, dq1], axis=1), dk1.at[:, :c].add(dk0), dv1.at[:, :c].add(dv0)


def _second_queries(q, do, lse, delta, k, v):
    c = q.shape[1] // 2
    scale = q.shape[-1] ** -0.5
    dq, dk, dv = _pair(q[:, c:], do[:, c:], lse[..., c:], delta[..., c:], k, v, None, scale)
    return jnp.concatenate([jnp.zeros_like(dq), dq], axis=1), dk, dv


def _first_keys(q, do, lse, delta, k, v):
    c = q.shape[1] // 2
    scale = q.shape[-1] ** -0.5
    dq, dk, dv = _pair(q, do, lse, delta, k[:, :c], v[:, :c], None, scale)
    return dq, jnp.concatenate([dk, jnp.zeros_like(dk)], axis=1), jnp.concatenate([dv, jnp.zeros_like(dv)], axis=1)


def solution(mesh):
    n = mesh.shape['cp']
    nxt = [(j, (j + 1) % n) for j in range(n)]
    spec = P('data', 'cp', None, None)
    lspec = P('data', None, 'cp')

    def local(q, k, v, o, lse, do):
        i = lax.axis_index('cp')
        delta = jnp.einsum('bqhd,bqhd->bhq', do, o, preferred_element_type=F32)
        dq, dk, dv = _same(q, do, lse, delta, k, v)
        qt, dot, lt, deltat = q, do, lse, delta
        for r in range(1, n):
            qt, dot, lt, deltat, dq = (lax.ppermute(x, 'cp', nxt) for x in (qt, dot, lt, deltat, dq))
            src = (i - r) % n
            ddq, ddk, ddv = lax.cond(src < i, _second_queries, _first_keys, qt, dot, lt, deltat, k, v)
            dq = dq + ddq
            dk = dk + ddk
            dv = dv + ddv
        dq = lax.ppermute(dq, 'cp', nxt)
        return dq.astype(BF16), dk.astype(BF16), dv.astype(BF16)

    return jax.shard_map(local, mesh=mesh, in_specs=(spec, spec, spec, spec, lspec, spec),
                         out_specs=(spec, spec, spec), check_vma=False)
```

profile of v0, /device:TPU:0, one launch (start us, length us, event | category | flops | bytes accessed | tf_op | source)
XLA Modules:
  0.0 5702.5 jit_solution(9244602881177935302)
XLA Ops:
  80.0 44.6 multiply_convert_fusion.14
  219.8 541.3 %collective-permute-done.2 = f32[1,96,512]{2,1,0:T(8,128)S(1)} collective-permute-done((f32[1,96,512]{2,1,0:T(8,128)S(1)}, f32[1,96,512]{2,1,0:T(8,128)S(1)}, u32[]{:S(2)}, u32[]{:S(2)}) %collective-permute-start.2) | collective-permute-done | bytes 196640 | tf_op jit(solution)/shard_map/ppermute | solution.py:59
  763.1 184.1 %conditional.7 = (f32[1,512,96,128]{3,1,2,0:T(8,128)}, f32[1,512,96,128]{3,1,2,0:T(8,128)}, f32[1,512,96,128]{3,1,2,0:T(8,128)}) conditional(s32[]{:T(128)} %convert_element_type.160, (bf16[1,512,96,128]{3,1,2,0:T(8,128)(2,1)}, bf16[1,512,96,128]{3,2,1,0:T(8,128)(2,1)}, f32[1,96,512]{2,1,0:T(8,128)S(1)}, bf16[1,512,96,128]{3,1,2,0:T(8,128)(2,1)}, ...), branch_computations={%region_0.1_spmd, %region_1.2_spmd} | conditional | flops 16216227840 | bytes 472449056 | solution.py:61
  808.4 29.4 multiply_convert_fusion
  973.1 545.1 %collective-permute-done.7 = f32[1,96,512]{2,1,0:T(8,128)S(1)} collective-permute-done((f32[1,96,512]{2,1,0:T(8,128)S(1)}, f32[1,96,512]{2,1,0:T(8,128)S(1)}, u32[]{:S(2)}, u32[]{:S(2)}) %collective-permute-start.7) | collective-permute-done | bytes 196640 | tf_op jit(solution)/shard_map/ppermute | solution.py:59
  1520.3 184.3 %conditional.8 = (f32[1,512,96,128]{3,1,2,0:T(8,128)}, f32[1,512,96,128]{3,1,2,0:T(8,128)}, f32[1,512,96,128]{3,1,2,0:T(8,128)}) conditional(s32[]{:T(128)} %convert_element_type.161, (bf16[1,512,96,128]{3,1,2,0:T(8,128)(2,1)}, bf16[1,512,96,128]{3,2,1,0:T(8,128)(2,1)}, f32[1,96,512]{2,1,0:T(8,128)S(1)}, bf16[1,512,96,128]{3,1,2,0:T(8,128)(2,1)}, ...), branch_computations={%region_2.3_spmd, %region_3.4_spmd} | conditional | flops 16216227840 | bytes 472449056 | solution.py:61
  1730.5 545.1 %collective-permute-done.12 = f32[1,96,512]{2,1,0:T(8,128)S(1)} collective-permute-done((f32[1,96,512]{2,1,0:T(8,128)S(1)}, f32[1,96,512]{2,1,0:T(8,128)S(1)}, u32[]{:S(2)}, u32[]{:S(2)}) %collective-permute-start.12) | collective-permute-done | bytes 196640 | tf_op jit(solution)/shard_map/ppermute | solution.py:59
  2277.8 183.8 %conditional.9 = (f32[1,512,96,128]{3,1,2,0:T(8,128)}, f32[1,512,96,128]{3,1,2,0:T(8,128)}, f32[1,512,96,128]{3,1,2,0:T(8,128)}) conditional(s32[]{:T(128)} %convert_element_type.162, (bf16[1,512,96,128]{3,1,2,0:T(8,128)(2,1)}, bf16[1,512,96,128]{3,2,1,0:T(8,128)(2,1)}, f32[1,96,512]{2,1,0:T(8,128)S(1)}, bf16[1,512,96,128]{3,1,2,0:T(8,128)(2,1)}, ...), branch_computations={%region_4.5_spmd, %region_5.6_spmd} | conditional | flops 16216227840 | bytes 472449056 | solution.py:61
  2322.8 29.3 multiply_convert_fusion.4
  2487.6 545.1 %collective-permute-done.17 = f32[1,96,512]{2,1,0:T(8,128)S(1)} collective-permute-done((f32[1,96,512]{2,1,0:T(8,128)S(1)}, f32[1,96,512]{2,1,0:T(8,128)S(1)}, u32[]{:S(2)}, u32[]{:S(2)}) %collective-permute-start.17) | collective-permute-done | bytes 196640 | tf_op jit(solution)/shard_map/ppermute | solution.py:59
  3034.8 184.2 %conditional.10 = (f32[1,512,96,128]{3,1,2,0:T(8,128)}, f32[1,512,96,128]{3,1,2,0:T(8,128)}, f32[1,512,96,128]{3,1,2,0:T(8,128)}) conditional(s32[]{:T(128)} %convert_element_type.163, (bf16[1,512,96,128]{3,1,2,0:T(8,128)(2,1)}, bf16[1,512,96,128]{3,2,1,0:T(8,128)(2,1)}, f32[1,96,512]{2,1,0:T(8,128)S(1)}, bf16[1,512,96,128]{3,1,2,0:T(8,128)(2,1)}, ...), branch_computations={%region_6.7_spmd, %region_7.8_spmd} | conditional | flops 16216227840 | bytes 472449056 | solution.py:61
  3079.9 29.4 multiply_convert_fusion.6
  3244.8 545.1 %collective-permute-done.22 = f32[1,96,512]{2,1,0:T(8,128)S(1)} collective-permute-done((f32[1,96,512]{2,1,0:T(8,128)S(1)}, f32[1,96,512]{2,1,0:T(8,128)S(1)}, u32[]{:S(2)}, u32[]{:S(2)}) %collective-permute-start.22) | collective-permute-done | bytes 196640 | tf_op jit(solution)/shard_map/ppermute | solution.py:59
  3792.1 184.4 %conditional.11 = (f32[1,512,96,128]{3,1,2,0:T(8,128)}, f32[1,512,96,128]{3,1,2,0:T(8,128)}, f32[1,512,96,128]{3,1,2,0:T(8,128)}) conditional(s32[]{:T(128)} %convert_element_type.164, (bf16[1,512,96,128]{3,1,2,0:T(8,128)(2,1)}, bf16[1,512,96,128]{3,2,1,0:T(8,128)(2,1)}, f32[1,96,512]{2,1,0:T(8,128)S(1)}, bf16[1,512,96,128]{3,1,2,0:T(8,128)(2,1)}, ...), branch_computations={%region_8.9_spmd, %region_9.10_spmd} | conditional | flops 16216227840 | bytes 472449056 | solution.py:61
  3837.1 29.4 multiply_convert_fusion.8
  4002.4 545.1 %collective-permute-done.27 = f32[1,96,512]{2,1,0:T(8,128)S(1)} collective-permute-done((f32[1,96,512]{2,1,0:T(8,128)S(1)}, f32[1,96,512]{2,1,0:T(8,128)S(1)}, u32[]{:S(2)}, u32[]{:S(2)}) %collective-permute-start.27) | collective-permute-done | bytes 196640 | tf_op jit(solution)/shard_map/ppermute | solution.py:59
  4549.7 184.2 %conditional.12 = (f32[1,512,96,128]{3,1,2,0:T(8,128)}, f32[1,512,96,128]{3,1,2,0:T(8,128)}, f32[1,512,96,128]{3,1,2,0:T(8,128)}) conditional(s32[]{:T(128)} %convert_element_type.165, (bf16[1,512,96,128]{3,1,2,0:T(8,128)(2,1)}, bf16[1,512,96,128]{3,2,1,0:T(8,128)(2,1)}, f32[1,96,512]{2,1,0:T(8,128)S(1)}, bf16[1,512,96,128]{3,1,2,0:T(8,128)(2,1)}, ...), branch_computations={%region_10.11_spmd, %region_11.12_spmd} | conditional | flops 16216227840 | bytes 472449056 | solution.py:61
  4594.7 29.3 multiply_convert_fusion.10
  4759.7 29.3 fusion.323
  4863.0 441.9 %collective-permute-done.32 = f32[1,96,512]{2,1,0:T(8,128)S(1)} collective-permute-done((f32[1,96,512]{2,1,0:T(8,128)S(1)}, f32[1,96,512]{2,1,0:T(8,128)S(1)}, u32[]{:S(2)}, u32[]{:S(2)}) %collective-permute-start.32) | collective-permute-done | bytes 196640 | tf_op jit(solution)/shard_map/ppermute | solution.py:59
  5307.1 184.0 %conditional.13 = (f32[1,512,96,128]{3,1,2,0:T(8,128)}, f32[1,512,96,128]{3,1,2,0:T(8,128)}, f32[1,512,96,128]{3,1,2,0:T(8,128)}) conditional(s32[]{:T(128)} %convert_element_type.166, (bf16[1,512,96,128]{3,1,2,0:T(8,128)(2,1)}, bf16[1,512,96,128]{3,2,1,0:T(8,128)(2,1)}, f32[1,96,512]{2,1,0:T(8,128)S(1)}, bf16[1,512,96,128]{3,1,2,0:T(8,128)(2,1)}, ...), branch_computations={%region_12.13_spmd, %region_13.14_spmd} | conditional | flops 16216227840 | bytes 472449056 | solution.py:61
  5352.5 29.4 multiply_convert_fusion.12
  5512.2 127.6 %add_convert_fusion = (bf16[1,512,96,128]{3,1,2,0:T(8,128)(2,1)}, bf16[1,512,96,128]{3,1,2,0:T(8,128)(2,1)}) fusion(f32[1,512,96,128]{3,1,2,0:T(8,128)} %get-tuple-element.320, f32[1,512,96,128]{3,1,2,0:T(8,128)} %get-tuple-element.319, f32[1,512,96,128]{3,1,2,0:T(8,128)} %get-tuple-element.318, f32[1,512,96,128]{3,1,2,0:T(8,128)} %get-tuple-element.317, ...), kind=kLoop, calls=%fused_computation.329 | loop fusion | flops 100663296 | bytes 427819008 | tf_op jit(solution)/shard_map/convert_element_type | solution.py:66
  5656.6 31.0 copy.82
  (196 shorter events, 1465.4 us)
Async XLA Ops:
  214.7 732.6 %collective-permute-start = (f32[1,512,96,128]{3,1,2,0:T(8,128)}, f32[1,512,96,128]{3,1,2,0:T(8,128)}, u32[]{:S(2)}, u32[]{:S(2)}) collective-permute-start(f32[1,512,96,128]{3,1,2,0:T(8,128)} %pad_maximum_fusion), channel_id=1, source_target_pairs={{0,1},{1,2},{2,3},{3,4},{4,5},{5,6},{6,7},{7,0}} | collective-permute-start | bytes 75497480 | tf_op jit(solution)/shard_map/ppermute | solution.py:59
  215.5 547.6 %collective-permute-start.1 = (bf16[1,512,96,128]{3,1,2,0:T(8,128)(2,1)}, bf16[1,512,96,128]{3,1,2,0:T(8,128)(2,1)}, u32[]{:S(2)}, u32[]{:S(2)}) collective-permute-start(bf16[1,512,96,128]{3,1,2,0:T(8,128)(2,1)} %copy.37), channel_id=1, source_target_pairs={{0,1},{1,2},{2,3},{3,4},{4,5},{5,6},{6,7},{7,0}} | collective-permute-start | bytes 37748744 | tf_op jit(solution)/shard_map/ppermute | solution.py:59
  972.9 731.7 %collective-permute-start.5 = (f32[1,512,96,128]{3,1,2,0:T(8,128)}, f32[1,512,96,128]{3,1,2,0:T(8,128)}, u32[]{:S(2)}, u32[]{:S(2)}) collective-permute-start(f32[1,512,96,128]{3,1,2,0:T(8,128)} %add.158), channel_id=1, source_target_pairs={{0,1},{1,2},{2,3},{3,4},{4,5},{5,6},{6,7},{7,0}} | collective-permute-start | bytes 75497480 | tf_op jit(solution)/shard_map/ppermute | solution.py:59
  972.9 547.4 %collective-permute-start.6 = (bf16[1,512,96,128]{3,1,2,0:T(8,128)(2,1)}, bf16[1,512,96,128]{3,1,2,0:T(8,128)(2,1)}, u32[]{:S(2)}, u32[]{:S(2)}) collective-permute-start(bf16[1,512,96,128]{3,1,2,0:T(8,128)(2,1)} %collective-permute-done.1), channel_id=1, source_target_pairs={{0,1},{1,2},{2,3},{3,4},{4,5},{5,6},{6,7},{7,0}} | collective-permute-start | bytes 37748744 | tf_op jit(solution)/shard_map/ppermute | solution.py:59
  972.9 547.4 %collective-permute-start.8 = (bf16[1,512,96,128]{3,1,2,0:T(8,128)(2,1)}, bf16[1,512,96,128]{3,1,2,0:T(8,128)(2,1)}, u32[]{:S(2)}, u32[]{:S(2)}) collective-permute-start(bf16[1,512,96,128]{3,1,2,0:T(8,128)(2,1)} %collective-permute-done.3), channel_id=1, source_target_pairs={{0,1},{1,2},{2,3},{3,4},{4,5},{5,6},{6,7},{7,0}} | collective-permute-start | bytes 37748744 | tf_op jit(solution)/shard_map/ppermute | solution.py:59
  1730.4 731.2 %collective-permute-start.10 = (f32[1,512,96,128]{3,1,2,0:T(8,128)}, f32[1,512,96,128]{3,1,2,0:T(8,128)}, u32[]{:S(2)}, u32[]{:S(2)}) collective-permute-start(f32[1,512,96,128]{3,1,2,0:T(8,128)} %add.160), channel_id=1, source_target_pairs={{0,1},{1,2},{2,3},{3,4},{4,5},{5,6},{6,7},{7,0}} | collective-permute-start | bytes 75497480 | tf_op jit(solution)/shard_map/ppermute | solution.py:59
  1730.4 547.4 %collective-permute-start.11 = (bf16[1,512,96,128]{3,1,2,0:T(8,128)(2,1)}, bf16[1,512,96,128]{3,1,2,0:T(8,128)(2,1)}, u32[]{:S(2)}, u32[]{:S(2)}) collective-permute-start(bf16[1,512,96,128]{3,1,2,0:T(8,128)(2,1)} %collective-permute-done.6), channel_id=1, source_target_pairs={{0,1},{1,2},{2,3},{3,4},{4,5},{5,6},{6,7},{7,0}} | collective-permute-start | bytes 37748744 | tf_op jit(solution)/shard_map/ppermute | solution.py:59
  1730.4 547.4 %collective-permute-start.13 = (bf16[1,512,96,128]{3,1,2,0:T(8,128)(2,1)}, bf16[1,512,96,128]{3,1,2,0:T(8,128)(2,1)}, u32[]{:S(2)}, u32[]{:S(2)}) collective-permute-start(bf16[1,512,96,128]{3,1,2,0:T(8,128)(2,1)} %collective-permute-done.8), channel_id=1, source_target_pairs={{0,1},{1,2},{2,3},{3,4},{4,5},{5,6},{6,7},{7,0}} | collective-permute-start | bytes 37748744 | tf_op jit(solution)/shard_map/ppermute | solution.py:59
  1730.5 547.3 %collective-permute-start.14 = (f32[1,96,512]{2,1,0:T(8,128)S(1)}, f32[1,96,512]{2,1,0:T(8,128)S(1)}, u32[]{:S(2)}, u32[]{:S(2)}) collective-permute-start(f32[1,96,512]{2,1,0:T(8,128)S(1)} %collective-permute-done.9), channel_id=1, source_target_pairs={{0,1},{1,2},{2,3},{3,4},{4,5},{5,6},{6,7},{7,0}} | collective-permute-start | bytes 589832 | tf_op jit(solution)/shard_map/ppermute | solution.py:59
  2487.4 731.6 %collective-permute-start.15 = (f32[1,512,96,128]{3,1,2,0:T(8,128)}, f32[1,512,96,128]{3,1,2,0:T(8,128)}, u32[]{:S(2)}, u32[]{:S(2)}) collective-permute-start(f32[1,512,96,128]{3,1,2,0:T(8,128)} %add.162), channel_id=1, source_target_pairs={{0,1},{1,2},{2,3},{3,4},{4,5},{5,6},{6,7},{7,0}} | collective-permute-start | bytes 75497480 | tf_op jit(solution)/shard_map/ppermute | solution.py:59
  2487.4 547.4 %collective-permute-start.16 = (bf16[1,512,96,128]{3,1,2,0:T(8,128)(2,1)}, bf16[1,512,96,128]{3,1,2,0:T(8,128)(2,1)}, u32[]{:S(2)}, u32[]{:S(2)}) collective-permute-start(bf16[1,512,96,128]{3,1,2,0:T(8,128)(2,1)} %collective-permute-done.11), channel_id=1, source_target_pairs={{0,1},{1,2},{2,3},{3,4},{4,5},{5,6},{6,7},{7,0}} | collective-permute-start | bytes 37748744 | tf_op jit(solution)/shard_map/ppermute | solution.py:59
  2487.4 547.4 %collective-permute-start.18 = (bf16[1,512,96,128]{3,1,2,0:T(8,128)(2,1)}, bf16[1,512,96,128]{3,1,2,0:T(8,128)(2,1)}, u32[]{:S(2)}, u32[]{:S(2)}) collective-permute-start(bf16[1,512,96,128]{3,1,2,0:T(8,128)(2,1)} %collective-permute-done.13), channel_id=1, source_target_pairs={{0,1},{1,2},{2,3},{3,4},{4,5},{5,6},{6,7},{7,0}} | collective-permute-start | bytes 37748744 | tf_op jit(solution)/shard_map/ppermute | solution.py:59
  2487.5 547.3 %collective-permute-start.19 = (f32[1,96,512]{2,1,0:T(8,128)S(1)}, f32[1,96,512]{2,1,0:T(8,128)S(1)}, u32[]{:S(2)}, u32[]{:S(2)}) collective-permute-start(f32[1,96,512]{2,1,0:T(8,128)S(1)} %collective-permute-done.14), channel_id=1, source_target_pairs={{0,1},{1,2},{2,3},{3,4},{4,5},{5,6},{6,7},{7,0}} | collective-permute-start | bytes 589832 | tf_op jit(solution)/shard_map/ppermute | solution.py:59
  3244.7 731.8 %collective-permute-start.20 = (f32[1,512,96,128]{3,1,2,0:T(8,128)}, f32[1,512,96,128]{3,1,2,0:T(8,128)}, u32[]{:S(2)}, u32[]{:S(2)}) collective-permute-start(f32[1,512,96,128]{3,1,2,0:T(8,128)} %add.164), channel_id=1, source_target_pairs={{0,1},{1,2},{2,3},{3,4},{4,5},{5,6},{6,7},{7,0}} | collective-permute-start | bytes 75497480 | tf_op jit(solution)/shard_map/ppermute | solution.py:59
  3244.7 547.4 %collective-permute-start.21 = (bf16[1,512,96,128]{3,1,2,0:T(8,128)(2,1)}, bf16[1,512,96,128]{3,1,2,0:T(8,128)(2,1)}, u32[]{:S(2)}, u32[]{:S(2)}) collective-permute-start(bf16[1,512,96,128]{3,1,2,0:T(8,128)(2,1)} %collective-permute-done.16), channel_id=1, source_target_pairs={{0,1},{1,2},{2,3},{3,4},{4,5},{5,6},{6,7},{7,0}} | collective-permute-start | bytes 37748744 | tf_op jit(solution)/shard_map/ppermute | solution.py:59
  3244.7 547.4 %collective-permute-start.23 = (bf16[1,512,96,128]{3,1,2,0:T(8,128)(2,1)}, bf16[1,512,96,128]{3,1,2,0:T(8,128)(2,1)}, u32[]{:S(2)}, u32[]{:S(2)}) collective-permute-start(bf16[1,512,96,128]{3,1,2,0:T(8,128)(2,1)} %collective-permute-done.18), channel_id=1, source_target_pairs={{0,1},{1,2},{2,3},{3,4},{4,5},{5,6},{6,7},{7,0}} | collective-permute-start | bytes 37748744 | tf_op jit(solution)/shard_map/ppermute | solution.py:59
  3244.8 547.3 %collective-permute-start.24 = (f32[1,96,512]{2,1,0:T(8,128)S(1)}, f32[1,96,512]{2,1,0:T(8,128)S(1)}, u32[]{:S(2)}, u32[]{:S(2)}) collective-permute-start(f32[1,96,512]{2,1,0:T(8,128)S(1)} %collective-permute-done.19), channel_id=1, source_target_pairs={{0,1},{1,2},{2,3},{3,4},{4,5},{5,6},{6,7},{7,0}} | collective-permute-start | bytes 589832 | tf_op jit(solution)/shard_map/ppermute | solution.py:59
  4002.3 731.6 %collective-permute-start.25 = (f32[1,512,96,128]{3,1,2,0:T(8,128)}, f32[1,512,96,128]{3,1,2,0:T(8,128)}, u32[]{:S(2)}, u32[]{:S(2)}) collective-permute-start(f32[1,512,96,128]{3,1,2,0:T(8,128)} %add.166), channel_id=1, source_target_pairs={{0,1},{1,2},{2,3},{3,4},{4,5},{5,6},{6,7},{7,0}} | collective-permute-start | bytes 75497480 | tf_op jit(solution)/shard_map/ppermute | solution.py:59
  4002.3 547.4 %collective-permute-start.26 = (bf16[1,512,96,128]{3,1,2,0:T(8,128)(2,1)}, bf16[1,512,96,128]{3,1,2,0:T(8,128)(2,1)}, u32[]{:S(2)}, u32[]{:S(2)}) collective-permute-start(bf16[1,512,96,128]{3,1,2,0:T(8,128)(2,1)} %collective-permute-done.21), channel_id=1, source_target_pairs={{0,1},{1,2},{2,3},{3,4},{4,5},{5,6},{6,7},{7,0}} | collective-permute-start | bytes 37748744 | tf_op jit(solution)/shard_map/ppermute | solution.py:59
  4002.3 547.4 %collective-permute-start.28 = (bf16[1,512,96,128]{3,1,2,0:T(8,128)(2,1)}, bf16[1,512,96,128]{3,1,2,0:T(8,128)(2,1)}, u32[]{:S(2)}, u32[]{:S(2)}) collective-permute-start(bf16[1,512,96,128]{3,1,2,0:T(8,128)(2,1)} %collective-permute-done.23), channel_id=1, source_target_pairs={{0,1},{1,2},{2,3},{3,4},{4,5},{5,6},{6,7},{7,0}} | collective-permute-start | bytes 37748744 | tf_op jit(solution)/shard_map/ppermute | solution.py:59
  4002.3 547.3 %collective-permute-start.29 = (f32[1,96,512]{2,1,0:T(8,128)S(1)}, f32[1,96,512]{2,1,0:T(8,128)S(1)}, u32[]{:S(2)}, u32[]{:S(2)}) collective-permute-start(f32[1,96,512]{2,1,0:T(8,128)S(1)} %collective-permute-done.24), channel_id=1, source_target_pairs={{0,1},{1,2},{2,3},{3,4},{4,5},{5,6},{6,7},{7,0}} | collective-permute-start | bytes 589832 | tf_op jit(solution)/shard_map/ppermute | solution.py:59
  4759.7 731.4 %collective-permute-start.30 = (f32[1,512,96,128]{3,1,2,0:T(8,128)}, f32[1,512,96,128]{3,1,2,0:T(8,128)}, u32[]{:S(2)}, u32[]{:S(2)}) collective-permute-start(f32[1,512,96,128]{3,1,2,0:T(8,128)} %add.168), channel_id=1, source_target_pairs={{0,1},{1,2},{2,3},{3,4},{4,5},{5,6},{6,7},{7,0}} | collective-permute-start | bytes 75497480 | tf_op jit(solution)/shard_map/ppermute | solution.py:59
  4759.7 547.4 %collective-permute-start.31 = (bf16[1,512,96,128]{3,1,2,0:T(8,128)(2,1)}, bf16[1,512,96,128]{3,1,2,0:T(8,128)(2,1)}, u32[]{:S(2)}, u32[]{:S(2)}) collective-permute-start(bf16[1,512,96,128]{3,1,2,0:T(8,128)(2,1)} %collective-permute-done.26), channel_id=1, source_target_pairs={{0,1},{1,2},{2,3},{3,4},{4,5},{5,6},{6,7},{7,0}} | collective-permute-start | bytes 37748744 | tf_op jit(solution)/shard_map/ppermute | solution.py:59
  4759.7 547.4 %collective-permute-start.33 = (bf16[1,512,96,128]{3,1,2,0:T(8,128)(2,1)}, bf16[1,512,96,128]{3,1,2,0:T(8,128)(2,1)}, u32[]{:S(2)}, u32[]{:S(2)}) collective-permute-start(bf16[1,512,96,128]{3,1,2,0:T(8,128)(2,1)} %collective-permute-done.28), channel_id=1, source_target_pairs={{0,1},{1,2},{2,3},{3,4},{4,5},{5,6},{6,7},{7,0}} | collective-permute-start | bytes 37748744 | tf_op jit(solution)/shard_map/ppermute | solution.py:59
  (33 other events, 6737.2 us)
where the time goes:
time: 5710 us; the launch traced here: 5700 us
  waiting for transfers between devices  3720 us (65%)
  matrix products  1050 us (18%)
  local copies, waits for them, and re-layouts  469 us (8%)
  other arithmetic  330 us (6%)
  loops' own time  118 us (2%)
    ppermute x35, waiting for transfers between devices, local(): lax.ppermute(x, 'cp', nxt)  3720 us
    dot_general x9, matrix products, _pair(): dp = jnp.einsum('bqhd,bkhd->bhqk', do, v, preferred_element_type=F32)  269 us
    dot_general x9, matrix products, _pair(): jnp.einsum('bhqk,bqhd->bkhd', p.astype(BF16), do, preferred_element_type=...  241 us
    dot_general x9, matrix products, _pair(): s = jnp.einsum('bqhd,bkhd->bhqk', q, k, preferred_element_type=F32) * scale  211 us
    add x7, other arithmetic, local(): dq = dq + ddq  176 us
    dot_general x9, matrix products, _pair(): jnp.einsum('bhqk,bqhd->bkhd', ds, q, preferred_element_type=F32) * scale  171 us
    dot_general x9, matrix products, _pair(): jnp.einsum('bhqk,bkhd->bqhd', ds, k, preferred_element_type=F32) * scale  163 us
    another operation x14, local copies, waits for them, and re-layouts  149 us
  transfers between devices with their start and end apart: 36, of which 14 were waited for; matrix products, arithmetic and copies ran while one was open for 25% of the time, Pallas kernels for 0%

commit v1 on v0

v1 whole, which is shorter than its diff:
```python
import functools

import jax
import jax.numpy as jnp
from jax import lax
from jax.experimental import pallas as pl
from jax.experimental.pallas import tpu as pltpu
from jax.sharding import PartitionSpec as P

F32 = jnp.float32
BF16 = jnp.bfloat16
MESH = pl.DeviceIdType.MESH

NT = (((1,), (1,)), ((), ()))
NN = (((1,), (0,)), ((), ()))


def _dot(a, b, dims):
    return lax.dot_general(a, b, dims, preferred_element_type=F32)


def _kernel(n, toks, heads, q_ref, k_ref, v_ref, o_ref, do_ref, lse_ref, dq_ref, dk_ref, dv_ref,
            raw, raw_lse, snd, snd_st, rcv, rcv_st, osnd, orcv, ostage, tmp, kt, dqt, dka, dva,
            isend, irecv, ssend, srecv, osend, orecv, ldsem, lsesem, stsem):
    half = toks // 2
    d = q_ref.shape[-1]
    scale = d ** -0.5
    chunks = heads // n
    me = lax.axis_index('cp')
    row = lax.axis_index('data')

    def peer(r):
        p = me
        if r & 1:
            p = p + 1 - 2 * lax.rem(me, 2)
        if r & 2:
            p = p + 2 - 4 * lax.rem(me // 2, 2)
        if r & 4:
            p = p + 4 - 8 * lax.rem(me // 4, 2)
        return p

    barrier = pltpu.get_barrier_semaphore()
    for r in range(1, n):
        pl.semaphore_signal(barrier, inc=1, device_id=(row, peer(r)), device_id_type=MESH)
    pl.semaphore_wait(barrier, n - 1)

    srcs = (q_ref, k_ref, v_ref, do_ref, o_ref)
    dsts = (dq_ref, dk_ref, dv_ref)

    def loads(c):
        h = pl.ds(pl.multiple_of(c * n, n), n)
        out = [pltpu.make_async_copy(x.at[:, h, :], raw.at[a], ldsem.at[a]) for a, x in enumerate(srcs)]
        out.append(pltpu.make_async_copy(lse_ref.at[h, :], raw_lse, lsesem))
        return out

    def stores(c):
        h = pl.ds(pl.multiple_of(c * n, n), n)
        return [pltpu.make_async_copy(ostage.at[a], x.at[:, h, :], stsem.at[a]) for a, x in enumerate(dsts)]

    def remote(src, dst, ssem, rsem, p):
        return pltpu.make_async_remote_copy(src_ref=src, dst_ref=dst, send_sem=ssem, recv_sem=rsem,
                                            device_id=(row, p), device_id_type=MESH)

    def in_copies(s, r, at):
        p = peer(r)
        a, b, par = lax.rem(s, 2), lax.rem(s, 3), lax.rem(s, 2)
        return (remote(snd.at[a, p], rcv.at[b, at], isend.at[r], irecv.at[par, r], p),
                remote(snd_st.at[a, p], rcv_st.at[b, at], ssend.at[r], srecv.at[par, r], p))

    def out_copies(s, r, at):
        p = peer(r)
        c = s - 2
        a, b, par = lax.rem(c, 2), lax.rem(c, 3), lax.rem(c, 2)
        return (remote(osnd.at[a, p], orcv.at[b, at], osend.at[r], orecv.at[par, r], p),)

    def prepare(c):
        a_slot = lax.rem(c, 2)
        part = toks // 4

        def tensor(a, _):
            def piece(i, _):
                rows = pl.ds(pl.multiple_of(i * part, part), part)
                x = raw[a, rows].astype(F32).reshape(part * n, d)
                tmp[pl.ds(0, part * n), :] = x
                for h in range(n):
                    snd[a_slot, h, pl.ds(pl.multiple_of(a * toks + i * part, part), part), :] = (
                        tmp[pl.ds(h, part, stride=n), :].astype(BF16))
                return 0
            return lax.fori_loop(0, 4, piece, 0)
        lax.fori_loop(0, 4, tensor, 0)

        def stat(i, _):
            rows = pl.ds(pl.multiple_of(i * part, part), part)
            x = raw[3, rows].astype(F32) * raw[4, rows].astype(F32)
            tmp[pl.ds(0, part * n), :] = x.reshape(part * n, d)
            for h in range(n):
                y = tmp[pl.ds(h, part, stride=n), :]
                snd_st[a_slot, h, 1:2, pl.ds(pl.multiple_of(i * part, part), part)] = (
                    jnp.sum(y.T, axis=0, keepdims=True))
            return 0
        lax.fori_loop(0, 4, stat, 0)
        for h in range(n):
            snd_st[a_slot, h, 0:1, :] = raw_lse[h:h + 1, :]

    def finalize(c):
        b_slot = lax.rem(c, 3)
        part = toks // 4

        def tensor(a, _):
            def piece(i, _):
                rows = pl.ds(pl.multiple_of(i * part, part), part)
                for h in range(n):
                    tmp[pl.ds(h, part, stride=n), :] = (
                        orcv[b_slot, h, pl.ds(pl.multiple_of(a * toks + i * part, part), part), :].astype(F32))
                ostage[a, rows] = tmp[pl.ds(0, part * n), :].reshape(part, n, d).astype(BF16)
                return 0
            return lax.fori_loop(0, 4, piece, 0)
        lax.fori_loop(0, 3, tensor, 0)

    def tile(b, i, q0, qn, j, k0, kn, mask):
        q = rcv[b, i, q0:q0 + qn, :]
        k = rcv[b, j, toks + k0:toks + k0 + kn, :]
        v = rcv[b, j, 2 * toks + k0:2 * toks + k0 + kn, :]
        do = rcv[b, i, 3 * toks + q0:3 * toks + q0 + qn, :]
        lse = rcv_st[b, i, 0:1, q0:q0 + qn]
        delta = rcv_st[b, i, 1:2, q0:q0 + qn]
        p = jnp.exp(_dot(k, q, NT) * scale - lse)
        if mask is not None:
            p = jnp.where(mask, p, 0.0)
        dp = _dot(v, do, NT)
        ds = (p * (dp - delta)).astype(BF16)
        dva[j, k0:k0 + kn, :] += _dot(p.astype(BF16), do, NN)
        dka[j, k0:k0 + kn, :] += _dot(ds, q, NN)
        dqt[i, :, q0:q0 + qn] += _dot(kt[j, :, k0:k0 + kn], ds, NN)

    def compute(c):
        b = lax.rem(c, 3)
        oslot = lax.rem(c, 2)

        def clear(j, _):
            kt[j] = rcv[b, j, toks:2 * toks, :].T
            dqt[j] = jnp.zeros((d, toks), F32)
            dka[j] = jnp.zeros((toks, d), F32)
            dva[j] = jnp.zeros((toks, d), F32)
            return 0
        lax.fori_loop(0, n, clear, 0)

        tri = (lax.broadcasted_iota(jnp.int32, (half, half), 0)
               <= lax.broadcasted_iota(jnp.int32, (half, half), 1))

        def keys(j, _):
            tile(b, j, 0, half, j, 0, half, tri)
            tile(b, j, half, half, j, 0, half, None)
            tile(b, j, half, half, j, half, half, tri)

            def lower(i, _):
                tile(b, i, half, half, j, 0, toks, None)
                return 0
            lax.fori_loop(0, j, lower, 0)

            def higher(i, _):
                tile(b, i, 0, toks, j, 0, half, None)
                return 0
            lax.fori_loop(j + 1, n, higher, 0)
            osnd[oslot, j, toks:2 * toks, :] = (dka[j] * scale).astype(BF16)
            osnd[oslot, j, 2 * toks:3 * toks, :] = dva[j].astype(BF16)
            return 0
        lax.fori_loop(0, n, keys, 0)

        def finish(i, _):
            osnd[oslot, i, 0:toks, :] = (dqt[i].T * scale).astype(BF16)
            return 0
        lax.fori_loop(0, n, finish, 0)

    for x in loads(0):
        x.start()
    for x in loads(0):
        x.wait()
    prepare(0)
    for x in loads(1):
        x.start()

    def step(s, _):
        sends_in = s < chunks
        sends_out = (s >= 2) & (s < chunks + 2)

        @pl.when(sends_in)
        def _():
            for r in (2, 4, 3, 5):
                for x in in_copies(s, r, me):
                    x.start()

        @pl.when(sends_out)
        def _():
            for r in (2, 4, 3, 5):
                for x in out_copies(s, r, me):
                    x.start()

        @pl.when(sends_in)
        def _():
            for r in (1, 6, 7):
                for x in in_copies(s, r, me):
                    x.start()
            a, b = lax.rem(s, 2), lax.rem(s, 3)
            rcv[b, me] = snd[a, me]
            rcv_st[b, me] = snd_st[a, me]

        @pl.when(sends_out)
        def _():
            for r in (1, 6, 7):
                for x in out_copies(s, r, me):
                    x.start()
            a, b = lax.rem(s - 2, 2), lax.rem(s - 2, 3)
            orcv[b, me] = osnd[a, me]

        @pl.when(s >= 4)
        def _():
            for x in stores(s - 4):
                x.start()

        @pl.when((s >= 1) & (s < chunks + 1))
        def _():
            compute(s - 1)

        @pl.when(s + 1 < chunks)
        def _():
            for x in loads(s + 1):
                x.wait()
            prepare(s + 1)

        @pl.when(s + 2 < chunks)
        def _():
            for x in loads(s + 2):
                x.start()

        @pl.when(s >= 4)
        def _():
            for x in stores(s - 4):
                x.wait()

        @pl.when(s >= 3)
        def _():
            finalize(s - 3)

        @pl.when(sends_in)
        def _():
            for r in range(1, n):
                for x in in_copies(s, r, me):
                    x.wait_send()
                for x in in_copies(s, r, peer(r)):
                    x.wait_recv()

        @pl.when(sends_out)
        def _():
            for r in range(1, n):
                for x in out_copies(s, r, me):
                    x.wait_send()
                for x in out_copies(s, r, peer(r)):
                    x.wait_recv()
        return 0

    lax.fori_loop(0, chunks + 3, step, 0)
    for x in stores(chunks - 1):
        x.start()
    for x in stores(chunks - 1):
        x.wait()


def solution(mesh):
    n = mesh.shape['cp']
    spec = P('data', 'cp', None, None)
    lspec = P('data', None, 'cp')

    def local(q, k, v, o, lse, do):
        _, toks, heads, d = q.shape
        out = jax.ShapeDtypeStruct((toks, heads, d), BF16)
        any_ = pl.BlockSpec(memory_space=pl.ANY)
        dma = pltpu.SemaphoreType.DMA
        dq, dk, dv = pl.pallas_call(
            functools.partial(_kernel, n, toks, heads),
            out_shape=(out, out, out),
            in_specs=[any_] * 6,
            out_specs=(any_,) * 3,
            scratch_shapes=[
                pltpu.VMEM((5, toks, n, d), BF16),
                pltpu.VMEM((n, toks), F32),
                pltpu.VMEM((2, n, 4 * toks, d), BF16),
                pltpu.VMEM((2, n, 2, toks), F32),
                pltpu.VMEM((3, n, 4 * toks, d), BF16),
                pltpu.VMEM((3, n, 2, toks), F32),
                pltpu.VMEM((2, n, 3 * toks, d), BF16),
                pltpu.VMEM((3, n, 3 * toks, d), BF16),
                pltpu.VMEM((3, toks, n, d), BF16),
                pltpu.VMEM((toks // 4 * n, d), F32),
                pltpu.VMEM((n, d, toks), BF16),
                pltpu.VMEM((n, d, toks), F32),
                pltpu.VMEM((n, toks, d), F32),
                pltpu.VMEM((n, toks, d), F32),
                dma((n,)), dma((2, n)), dma((n,)), dma((2, n)), dma((n,)), dma((2, n)),
                dma((5,)), dma, dma((3,)),
            ],
            compiler_params=pltpu.CompilerParams(
                collective_id=0, has_side_effects=True, vmem_limit_bytes=67_043_328),
        )(q[0], k[0], v[0], o[0], do[0], lse[0])
        return dq[None], dk[None], dv[None]

    return jax.shard_map(local, mesh=mesh, in_specs=(spec, spec, spec, spec, lspec, spec),
                         out_specs=(spec, spec, spec), check_vma=False)
```

time: 5710 us -> 1030 us (0.18)
  waiting for transfers between devices: 3720 us -> 0 us
  matrix products: 1050 us -> 0 us
  Pallas kernels: 0 us -> 999 us
  local copies, waits for them, and re-layouts: 469 us -> 26.1 us
  other arithmetic: 330 us -> 0.01 us
  loops' own time: 118 us -> 0 us
    ppermute x36 -> x0, waiting for transfers between devices: 3720 us -> none  [the longest x35 3720 us: local(): lax.ppermute(x, 'cp', nxt)]
    dot_general x45 -> x0, matrix products: 1050 us -> none  [the longest x9 269 us: _pair(): dp = jnp.einsum('bqhd,bkhd->bhqk', do, v, preferred_element_type=F32)]
    pallas_call x0 -> x1, Pallas kernels: none -> 999 us  [local(): pl.pallas_call(functools.partial(_kernel, n, toks, heads), out_shape=(out...]
    concatenate x15 -> x0, local copies, waits for them, and re-layouts: 198 us -> none  [the longest x7 99.5 us: _first_keys(): jnp.concatenate([dv, jnp.zeros_like(dv)], axis=1)]
    add x7 -> x0, other arithmetic: 176 us -> none  [local(): dq = dq + ddq]
    another operation x14 -> x0, local copies, waits for them, and re-layouts: 149 us -> none
    convert_element_type x1 -> x0, other arithmetic: 128 us -> none  [local(): return (dq.astype(BF16), dk.astype(BF16), dv.astype(BF16))]
    another operation x7 -> x0, loops' own time: 118 us -> none  [local(): lax.cond(src < i, _second_queries, _first_keys, qt, dot, lt, deltat, k, v)]
  transfers between devices with their start and end apart: 36 -> 0, of which waited for: 14 -> 0; matrix products, arithmetic and copies ran while one was open for 25% -> 0% of each run, Pallas kernels for 0% -> 0%
where the time goes in v1:
time: 1030 us
  Pallas kernels  999 us (97%)
  local copies, waits for them, and re-layouts  26.1 us (3%)
    pallas_call x1, Pallas kernels, local(): pl.pallas_call(functools.partial(_kernel, n, toks, heads), out_shape=(out...  999 us
    unnamed x11, local copies, waits for them, and re-layouts  26.1 us

profile of v1, /device:TPU:0, one launch (start us, length us, event | category | flops | bytes accessed | tf_op | source)
XLA Modules:
  0.0 1025.6 jit_solution(1614332719680016907)
XLA Ops:
  0.6 998.8 %shard_map.85 = (bf16[512,96,128]{2,1,0:T(8,128)(2,1)}, bf16[512,96,128]{2,1,0:T(8,128)(2,1)}, bf16[512,96,128]{2,1,0:T(8,128)(2,1)}) custom-call(bf16[512,96,128]{2,1,0:T(8,128)(2,1)} %bitcast.14, bf16[512,96,128]{2,1,0:T(8,128)(2,1)} %bitcast.15, bf16[512,96,128]{2,1,0:T(8,128)(2,1)} %bitcast.16, bf16[512,96,128]{2,1,0:T(8,128)(2,1)} %bitcast.17, ...), custom_call_target="tpu_custom_call" | custom-call | tf_op jit(solution)/shard_map/pallas_call | solution.py:279
  999.5 0.0 copy-start
  999.5 0.0 slice-start
  999.5 0.0 slice-start.1
  999.5 13.0 %copy.12 = bf16[1,512,96,128]{3,2,1,0:T(8,128)(2,1)} copy(bf16[1,512,96,128]{3,2,1,0:T(8,128)(2,1)} %bitcast.13) | data formatting | bytes 25165824
  1012.5 0.0 copy-done
  1012.5 0.0 slice-start.2
  1012.5 6.4 copy.13
  1018.9 0.0 slice-done
  1018.9 0.0 slice-done.1
  1018.9 1.9 slice-done.2
  1020.8 4.8 copy.14
  (1 shorter events, 0.0 us)
Async XLA Ops:
  999.5 13.1 %copy-start = (bf16[512,96,128]{2,1,0:T(8,128)(2,1)S(1)}, bf16[512,96,128]{2,1,0:T(8,128)(2,1)}, u32[]{:S(2)}) copy-start(bf16[512,96,128]{2,1,0:T(8,128)(2,1)} %get-tuple-element.7) | copy-start | bytes 37748740
  999.5 19.4 %slice-start = ((s8[12582912]{0:T(1024)(128)(4,1)}), s8[4194304]{0:T(1024)(128)(4,1)S(1)}, s32[]{:S(2)}) async-start(s8[12582912]{0:T(1024)(128)(4,1)} %bitcast.9), calls=%async_computation | async-start | bytes 8388608
  999.5 19.4 %slice-start.1 = ((s8[12582912]{0:T(1024)(128)(4,1)}), s8[4194304]{0:T(1024)(128)(4,1)S(1)}, s32[]{:S(2)}) async-start(s8[12582912]{0:T(1024)(128)(4,1)} %bitcast.9), calls=%async_computation.1 | async-start | bytes 8388608
  1012.5 8.3 slice-start.2

commit v2 on v1

--- a/solution.py
+++ b/solution.py
@@ -39,11 +39,6 @@
             p = p + 4 - 8 * lax.rem(me // 4, 2)
         return p
 
-    barrier = pltpu.get_barrier_semaphore()
-    for r in range(1, n):
-        pl.semaphore_signal(barrier, inc=1, device_id=(row, peer(r)), device_id_type=MESH)
-    pl.semaphore_wait(barrier, n - 1)
-
     srcs = (q_ref, k_ref, v_ref, do_ref, o_ref)
     dsts = (dq_ref, dk_ref, dv_ref)
 
@@ -67,9 +62,8 @@
         return (remote(snd.at[a, p], rcv.at[b, at], isend.at[r], irecv.at[par, r], p),
                 remote(snd_st.at[a, p], rcv_st.at[b, at], ssend.at[r], srecv.at[par, r], p))
 
-    def out_copies(s, r, at):
+    def out_copies(c, r, at):
         p = peer(r)
-        c = s - 2
         a, b, par = lax.rem(c, 2), lax.rem(c, 3), lax.rem(c, 2)
         return (remote(osnd.at[a, p], orcv.at[b, at], osend.at[r], orecv.at[par, r], p),)
 
@@ -133,9 +127,8 @@
         dka[j, k0:k0 + kn, :] += _dot(ds, q, NN)
         dqt[i, :, q0:q0 + qn] += _dot(kt[j, :, k0:k0 + kn], ds, NN)
 
-    def compute(c):
+    def begin(c):
         b = lax.rem(c, 3)
-        oslot = lax.rem(c, 2)
 
         def clear(j, _):
             kt[j] = rcv[b, j, toks:2 * toks, :].T
@@ -145,6 +138,8 @@
             return 0
         lax.fori_loop(0, n, clear, 0)
 
+    def compute(c, lo, hi):
+        b = lax.rem(c, 3)
         tri = (lax.broadcasted_iota(jnp.int32, (half, half), 0)
                <= lax.broadcasted_iota(jnp.int32, (half, half), 1))
 
@@ -162,65 +157,95 @@
                 tile(b, i, 0, toks, j, 0, half, None)
                 return 0
             lax.fori_loop(j + 1, n, higher, 0)
-            osnd[oslot, j, toks:2 * toks, :] = (dka[j] * scale).astype(BF16)
-            osnd[oslot, j, 2 * toks:3 * toks, :] = dva[j].astype(BF16)
             return 0
-        lax.fori_loop(0, n, keys, 0)
-
-        def finish(i, _):
+        lax.fori_loop(lo, hi, keys, 0)
+
+    def finish(c):
+        oslot = lax.rem(c, 2)
+
+        def block(i, _):
             osnd[oslot, i, 0:toks, :] = (dqt[i].T * scale).astype(BF16)
+            osnd[oslot, i, toks:2 * toks, :] = (dka[i] * scale).astype(BF16)
+            osnd[oslot, i, 2 * toks:3 * toks, :] = dva[i].astype(BF16)
             return 0
-        lax.fori_loop(0, n, finish, 0)
+        lax.fori_loop(0, n, block, 0)
 
     for x in loads(0):
         x.start()
+    barrier = pltpu.get_barrier_semaphore()
+    for r in range(1, n):
+        pl.semaphore_signal(barrier, inc=1, device_id=(row, peer(r)), device_id_type=MESH)
     for x in loads(0):
         x.wait()
     prepare(0)
     for x in loads(1):
         x.start()
+    pl.semaphore_wait(barrier, n - 1)
+
+    order = (2, 4, 3, 5, 1, 6, 7)
+
+    def begin_in(s):
+        for r in order:
+            for x in in_copies(s, r, me):
+                x.start()
+        a, b = lax.rem(s, 2), lax.rem(s, 3)
+        rcv[b, me] = snd[a, me]
+        rcv_st[b, me] = snd_st[a, me]
+
+    def end_in(s):
+        for r in range(1, n):
+            for x in in_copies(s, r, me):
+                x.wait_send()
+            for x in in_copies(s, r, peer(r)):
+                x.wait_recv()
+
+    def begin_out(c):
+        for r in order:
+            for x in out_copies(c, r, me):
+                x.start()
+        a, b = lax.rem(c, 2), lax.rem(c, 3)
+        orcv[b, me] = osnd[a, me]
+
+    def end_out(c):
+        for r in range(1, n):
+            for x in out_copies(c, r, me):
+                x.wait_send()
+            for x in out_copies(c, r, peer(r)):
+                x.wait_recv()
 
     def step(s, _):
-        sends_in = s < chunks
-        sends_out = (s >= 2) & (s < chunks + 2)
-
-        @pl.when(sends_in)
-        def _():
-            for r in (2, 4, 3, 5):
-                for x in in_copies(s, r, me):
-                    x.start()
-
-        @pl.when(sends_out)
-        def _():
-            for r in (2, 4, 3, 5):
-                for x in out_copies(s, r, me):
-                    x.start()
-
-        @pl.when(sends_in)
-        def _():
-            for r in (1, 6, 7):
-                for x in in_copies(s, r, me):
-                    x.start()
-            a, b = lax.rem(s, 2), lax.rem(s, 3)
-            rcv[b, me] = snd[a, me]
-            rcv_st[b, me] = snd_st[a, me]
-
-        @pl.when(sends_out)
-        def _():
-            for r in (1, 6, 7):
-                for x in out_copies(s, r, me):
-                    x.start()
-            a, b = lax.rem(s - 2, 2), lax.rem(s - 2, 3)
-            orcv[b, me] = osnd[a, me]
+        computes = (s >= 1) & (s < chunks + 1)
+
+        @pl.when(computes)
+        def _():
+            end_in(s - 1)
+
+        @pl.when(s < chunks)
+        def _():
+            begin_in(s)
 
         @pl.when(s >= 4)
         def _():
             for x in stores(s - 4):
                 x.start()
 
-        @pl.when((s >= 1) & (s < chunks + 1))
-        def _():
-            compute(s - 1)
+        @pl.when(computes)
+        def _():
+            begin(s - 1)
+            compute(s - 1, 0, n // 2)
+
+        @pl.when(s >= 3)
+        def _():
+            end_out(s - 3)
+
+        @pl.when((s >= 2) & (s < chunks + 2))
+        def _():
+            begin_out(s - 2)
+
+        @pl.when(computes)
+        def _():
+            compute(s - 1, n // 2, n)
+            finish(s - 1)
 
         @pl.when(s + 1 < chunks)
         def _():
@@ -241,22 +266,6 @@
         @pl.when(s >= 3)
         def _():
             finalize(s - 3)
-
-        @pl.when(sends_in)
-        def _():
-            for r in range(1, n):
-                for x in in_copies(s, r, me):
-                    x.wait_send()
-                for x in in_copies(s, r, peer(r)):
-                    x.wait_recv()
-
-        @pl.when(sends_out)
-        def _():
-            for r in range(1, n):
-                for x in out_copies(s, r, me):
-                    x.wait_send()
-                for x in out_copies(s, r, peer(r)):
-                    x.wait_recv()
         return 0
 
     lax.fori_loop(0, chunks + 3, step, 0)

time: 1030 us -> 999 us (0.970)
  Pallas kernels: 999 us -> 971 us
    pallas_call x1, Pallas kernels: 999 us -> 971 us  [local(): pl.pallas_call(functools.partial(_kernel, n, toks, heads), out_shape=(out...]
where the time goes in v2:
time: 999 us; the launch traced here: 998 us
  Pallas kernels  971 us (97%)
  local copies, waits for them, and re-layouts  26.1 us (3%)
    pallas_call x1, Pallas kernels, local(): pl.pallas_call(functools.partial(_kernel, n, toks, heads), out_shape=(out...  971 us
    unnamed x11, local copies, waits for them, and re-layouts  26.1 us

profile of v2, /device:TPU:0, one launch (start us, length us, event | category | flops | bytes accessed | tf_op | source)
XLA Modules:
  0.0 998.3 jit_solution(8246457683588788059)
XLA Ops:
  0.6 971.5 %shard_map.85 = (bf16[512,96,128]{2,1,0:T(8,128)(2,1)}, bf16[512,96,128]{2,1,0:T(8,128)(2,1)}, bf16[512,96,128]{2,1,0:T(8,128)(2,1)}) custom-call(bf16[512,96,128]{2,1,0:T(8,128)(2,1)} %bitcast.14, bf16[512,96,128]{2,1,0:T(8,128)(2,1)} %bitcast.15, bf16[512,96,128]{2,1,0:T(8,128)(2,1)} %bitcast.16, bf16[512,96,128]{2,1,0:T(8,128)(2,1)} %bitcast.17, ...), custom_call_target="tpu_custom_call" | custom-call | tf_op jit(solution)/shard_map/pallas_call | solution.py:288
  972.1 0.0 copy-start
  972.1 0.0 slice-start
  972.2 0.0 slice-start.1
  972.2 13.0 %copy.12 = bf16[1,512,96,128]{3,2,1,0:T(8,128)(2,1)} copy(bf16[1,512,96,128]{3,2,1,0:T(8,128)(2,1)} %bitcast.13) | data formatting | bytes 25165824
  985.2 0.0 copy-done
  985.2 0.0 slice-start.2
  985.2 6.4 copy.13
  991.6 0.0 slice-done
  991.6 0.0 slice-done.1
  991.6 1.9 slice-done.2
  993.5 4.8 copy.14
  (1 shorter events, 0.0 us)
Async XLA Ops:
  972.1 13.1 %copy-start = (bf16[512,96,128]{2,1,0:T(8,128)(2,1)S(1)}, bf16[512,96,128]{2,1,0:T(8,128)(2,1)}, u32[]{:S(2)}) copy-start(bf16[512,96,128]{2,1,0:T(8,128)(2,1)} %get-tuple-element.7) | copy-start | bytes 37748740
  972.1 19.4 %slice-start = ((s8[12582912]{0:T(1024)(128)(4,1)}), s8[4194304]{0:T(1024)(128)(4,1)S(1)}, s32[]{:S(2)}) async-start(s8[12582912]{0:T(1024)(128)(4,1)} %bitcast.9), calls=%async_computation | async-start | bytes 8388608
  972.2 19.4 %slice-start.1 = ((s8[12582912]{0:T(1024)(128)(4,1)}), s8[4194304]{0:T(1024)(128)(4,1)S(1)}, s32[]{:S(2)}) async-start(s8[12582912]{0:T(1024)(128)(4,1)} %bitcast.9), calls=%async_computation.1 | async-start | bytes 8388608
  985.2 8.3 slice-start.2
